TPU v7x, 32 devices: a whole 2x2x4 slice. The times are simulated.
32 devices in a mesh: dp: 8 (over z, y), tp: 4 (over x, core).
Axes of the slice: x: 2, y: 2, z: 4, core: 2. Of those that a mesh axis runs over, the one named last changes fastest.
Arguments:
- activations: bfloat16 [16, 256, 768], P('dp', 'tp'), may hold values from -6 to 6
- pair_rep: bfloat16 [16, 256, 256, 256], P('dp', 'tp'), may hold values from -6 to 6
- noise_times: float32 [16], P('dp'), may hold values from 0 to 1
- class_ids: int32 [16], P('dp'), may hold values from 0 to 40
- chain_lengths: int32 [16], P('dp'), may hold values from 64 to 256, as said below
- ada_weight: bfloat16 [256, 4608], replicated, may hold values from -0.375 to 0.375
- class_table: bfloat16 [41, 256], replicated, may hold values from -4 to 4
- pair_weight: bfloat16 [12, 256], replicated, may hold values from -0.375 to 0.375
- attn_in: bfloat16 [4, 768, 768], P(None, None, 'tp'), may hold values from -0.21875 to 0.21875
- attn_out: bfloat16 [768, 768], P('tp'), may hold values from -2.5 to 2.5
- ff_in: bfloat16 [2, 768, 3072], P(None, None, 'tp'), may hold values from -0.21875 to 0.21875
- ff_out: bfloat16 [3072, 768], P('tp'), may hold values from -0.109375 to 0.109375
- cotangent: bfloat16 [16, 256, 768], P('dp', 'tp'), may hold values from -6 to 6
Outputs:
- result: bfloat16 [16, 256, 768], P('dp', 'tp')
- grad_inputs: bfloat16 [16, 256, 768], P('dp', 'tp')
- grad_pair: bfloat16 [16, 256, 256, 256], P('dp', 'tp')
- grad_attn_in: float32 [4, 768, 768], P(None, 'dp', 'tp')
- grad_attn_out: float32 [768, 768], P('tp', 'dp')
- grad_ff_in: float32 [2, 768, 3072], P(None, 'dp', 'tp')
- grad_ff_out: float32 [3072, 768], P('tp', 'dp')
- grad_ada: float32 [256, 4608], P(None, 'dp')
- grad_table: float32 [41, 256], P(None, 'dp')
- grad_pair_weight: float32 [12, 256], P(None, 'dp')
Inputs may be any that keep to these rules, and one draw needn't show every extreme that they name: `chain_lengths`: every chain has at least a quarter of its 256 slots valid, and in each draw some chain has all 256.
All inputs are finite; a program needn't handle non-finite values.
Results may differ from a plain program's by a relative error of at most 0.02.
The roundings to bfloat16 on the way count: a program that leaves them out, or rounds other values in their place, can miss the bound.
Values may be sent and summed in bfloat16 or wider, within the bound.
A program may use at most 128 MiB of HBM per device.

v0:
```python
import math
import jax
import jax.numpy as jnp
from jax import lax
from jax.sharding import PartitionSpec as P

highest = lax.Precision.HIGHEST


def time_features(noise_times, cond_width):
    half_width = cond_width // 2
    freq_steps = jnp.arange(half_width).astype(jnp.float32)
    frequency = jnp.exp(freq_steps * (-math.log(10000.0) / half_width))
    angles = 100.0 * noise_times[:, None] * frequency[None, :]
    return jnp.concatenate([jnp.sin(angles), jnp.cos(angles)], axis=1)


def normalize(rows_in):
    centered = rows_in - jnp.mean(rows_in, axis=-1, keepdims=True)
    inverse = lax.rsqrt(jnp.mean(centered * centered, axis=-1, keepdims=True) + 1e-05)
    return (centered * inverse, inverse)


def norm_back(grad_rows, normed, inverse):
    mean_grad = jnp.mean(grad_rows, axis=-1, keepdims=True)
    mean_cross = jnp.mean(grad_rows * normed, axis=-1, keepdims=True)
    return inverse * (grad_rows - mean_grad - normed * mean_cross)


def row_sums(values):
    return jnp.sum(values, axis=1)


def local(
    activations,
    pair_rep,
    noise_times,
    class_ids,
    chain_lengths,
    ada_weight,
    class_table,
    pair_weight,
    attn_in,
    attn_out,
    ff_in,
    ff_out,
    cotangent,
):
    chains, local_rows, width = activations.shape
    length = pair_rep.shape[2]
    heads_here = pair_weight.shape[0] // lax.axis_size("tp")
    head_local = attn_in.shape[2]
    head_width = head_local // heads_here
    score_scale = head_width ** (-0.5)
    head_shape = (chains, length, heads_here, head_width)
    onehot = (class_ids[:, None] == jnp.arange(class_table.shape[0])[None, :]).astype(jnp.float32)
    table_full = class_table.astype(jnp.float32)
    ada_full = ada_weight.astype(jnp.float32)
    condition = time_features(noise_times, class_table.shape[1]) + jnp.dot(
        onehot, table_full, precision=highest
    )
    modulation = jnp.dot(condition, ada_full, precision=highest)
    pieces = [modulation[:, entry * width : (entry + 1) * width][:, None, :] for entry in range(6)]
    scale_attn, shift_attn, gate_attn, scale_ff, shift_ff, gate_ff = pieces
    inputs_full = activations.astype(jnp.float32)
    normed_attn, inverse_attn = normalize(inputs_full)
    rows_attn = (normed_attn * (1.0 + scale_attn) + shift_attn).astype(jnp.bfloat16)
    gathered_attn = lax.all_gather(rows_attn, "tp", axis=1, tiled=True)
    projected = jnp.einsum(
        "gld,kde->kgle", gathered_attn, attn_in, preferred_element_type=jnp.float32
    )
    query = projected[0].astype(jnp.bfloat16).reshape(head_shape)
    key_rows = projected[1].astype(jnp.bfloat16).reshape(head_shape)
    value_rows = projected[2].astype(jnp.bfloat16).reshape(head_shape)
    gate_pre = projected[3]
    bias_local = jnp.einsum(
        "gqkp,hp->ghqk", pair_rep, pair_weight, preferred_element_type=jnp.float32
    ).astype(jnp.bfloat16)
    pair_bias = lax.all_to_all(bias_local, "tp", split_axis=1, concat_axis=2, tiled=True)
    key_valid = (jnp.arange(length)[None, :] < chain_lengths[:, None])[:, None, None, :]

    def masked_scores():
        raw_scores = jnp.einsum(
            "gqhe,gkhe->ghqk", query, key_rows, preferred_element_type=jnp.float32
        ) * score_scale + pair_bias.astype(jnp.float32)
        return jnp.where(key_valid, raw_scores, -1e30)

    scores = masked_scores()
    row_top = jnp.max(scores, axis=-1, keepdims=True)
    log_total = row_top + jnp.log(jnp.sum(jnp.exp(scores - row_top), axis=-1, keepdims=True))
    soft_low = jnp.exp(scores - log_total).astype(jnp.bfloat16)
    head_mix = jnp.einsum(
        "ghqk,gkhe->gqhe", soft_low, value_rows, preferred_element_type=jnp.float32
    ).reshape(chains, length, head_local)
    gate_sig = jax.nn.sigmoid(gate_pre)
    gated_mix = (head_mix * gate_sig).astype(jnp.bfloat16)
    attn_terms = jnp.einsum("gle,ed->gld", gated_mix, attn_out, preferred_element_type=jnp.float32)
    attended = lax.psum_scatter(
        attn_terms.astype(jnp.bfloat16), "tp", scatter_dimension=1, tiled=True
    ).astype(jnp.float32)
    sig_attn = jax.nn.sigmoid(gate_attn)
    middle = inputs_full + sig_attn * attended
    normed_ff, inverse_ff = normalize(middle)
    rows_ff = (normed_ff * (1.0 + scale_ff) + shift_ff).astype(jnp.bfloat16)
    gathered_ff = lax.all_gather(rows_ff, "tp", axis=1, tiled=True)
    gate_up = jnp.einsum("gld,kdf->kglf", gathered_ff, ff_in, preferred_element_type=jnp.float32)
    sig_hidden = jax.nn.sigmoid(gate_up[0])
    silu_hidden = gate_up[0] * sig_hidden
    hidden = (silu_hidden * gate_up[1]).astype(jnp.bfloat16)
    ff_terms = jnp.einsum("glf,fd->gld", hidden, ff_out, preferred_element_type=jnp.float32)
    transition = lax.psum_scatter(
        ff_terms.astype(jnp.bfloat16), "tp", scatter_dimension=1, tiled=True
    ).astype(jnp.float32)
    sig_ff = jax.nn.sigmoid(gate_ff)
    result = (middle + sig_ff * transition).astype(jnp.bfloat16)
    upstream = cotangent.astype(jnp.float32)
    grad_trans = (sig_ff * upstream).astype(jnp.bfloat16)
    grad_gate_ff = row_sums(upstream * transition) * (sig_ff * (1.0 - sig_ff))[:, 0, :]
    gathered_grad_ff = lax.all_gather(grad_trans, "tp", axis=1, tiled=True)
    grad_ff_out = jnp.einsum(
        "glf,gld->fd", hidden, gathered_grad_ff, preferred_element_type=jnp.float32
    )
    grad_hidden = jnp.einsum(
        "gld,fd->glf", gathered_grad_ff, ff_out, preferred_element_type=jnp.float32
    )
    silu_slope = sig_hidden * (1.0 + gate_up[0] * (1.0 - sig_hidden))
    grad_gate_up = jnp.stack(
        [grad_hidden * gate_up[1] * silu_slope, grad_hidden * silu_hidden]
    ).astype(jnp.bfloat16)
    grad_ff_in = jnp.einsum(
        "gld,kglf->kdf", gathered_ff, grad_gate_up, preferred_element_type=jnp.float32
    )
    ff_row_terms = jnp.einsum(
        "kglf,kdf->gld", grad_gate_up, ff_in, preferred_element_type=jnp.float32
    )
    grad_rows_ff = lax.psum_scatter(
        ff_row_terms.astype(jnp.bfloat16), "tp", scatter_dimension=1, tiled=True
    ).astype(jnp.float32)
    grad_scale_ff = row_sums(grad_rows_ff * normed_ff)
    grad_shift_ff = row_sums(grad_rows_ff)
    grad_middle = upstream + norm_back(grad_rows_ff * (1.0 + scale_ff), normed_ff, inverse_ff)
    grad_attended = (sig_attn * grad_middle).astype(jnp.bfloat16)
    grad_gate_attn = row_sums(grad_middle * attended) * (sig_attn * (1.0 - sig_attn))[:, 0, :]
    gathered_grad_attn = lax.all_gather(grad_attended, "tp", axis=1, tiled=True)
    grad_attn_out = jnp.einsum(
        "gle,gld->ed", gated_mix, gathered_grad_attn, preferred_element_type=jnp.float32
    )
    grad_gated = jnp.einsum(
        "gld,ed->gle", gathered_grad_attn, attn_out, preferred_element_type=jnp.float32
    )
    grad_mix = (grad_gated * gate_sig).astype(jnp.bfloat16)
    grad_gate_pre = (grad_gated * head_mix * gate_sig * (1.0 - gate_sig)).astype(jnp.bfloat16)
    grad_mix_heads = grad_mix.reshape(head_shape)
    soft_full = jnp.exp(masked_scores() - log_total)
    grad_soft = jnp.einsum(
        "gqhe,gkhe->ghqk", grad_mix_heads, value_rows, preferred_element_type=jnp.float32
    )
    grad_scores = (
        soft_full * (grad_soft - jnp.sum(grad_soft * soft_full, axis=-1, keepdims=True))
    ).astype(jnp.bfloat16)
    grad_query = (
        jnp.einsum("ghqk,gkhe->gqhe", grad_scores, key_rows, preferred_element_type=jnp.float32)
        * score_scale
    ).astype(jnp.bfloat16)
    grad_key = (
        jnp.einsum("ghqk,gqhe->gkhe", grad_scores, query, preferred_element_type=jnp.float32)
        * score_scale
    ).astype(jnp.bfloat16)
    grad_value = jnp.einsum(
        "ghqk,gqhe->gkhe", soft_low, grad_mix_heads, preferred_element_type=jnp.float32
    ).astype(jnp.bfloat16)
    flat_shape = (chains, length, head_local)
    grad_heads = jnp.stack(
        [
            grad_query.reshape(flat_shape),
            grad_key.reshape(flat_shape),
            grad_value.reshape(flat_shape),
            grad_gate_pre,
        ]
    )
    grad_attn_in = jnp.einsum(
        "gld,kgle->kde", gathered_attn, grad_heads, preferred_element_type=jnp.float32
    )
    attn_row_terms = jnp.einsum(
        "kgle,kde->gld", grad_heads, attn_in, preferred_element_type=jnp.float32
    )
    grad_rows_attn = lax.psum_scatter(
        attn_row_terms.astype(jnp.bfloat16), "tp", scatter_dimension=1, tiled=True
    ).astype(jnp.float32)
    grad_scale_attn = row_sums(grad_rows_attn * normed_attn)
    grad_shift_attn = row_sums(grad_rows_attn)
    grad_inputs = (
        grad_middle + norm_back(grad_rows_attn * (1.0 + scale_attn), normed_attn, inverse_attn)
    ).astype(jnp.bfloat16)
    bias_grads = lax.all_to_all(grad_scores, "tp", split_axis=2, concat_axis=1, tiled=True)
    grad_pair = jnp.einsum(
        "ghqk,hp->gqkp", bias_grads, pair_weight, preferred_element_type=jnp.float32
    ).astype(jnp.bfloat16)
    pair_weight_part = jnp.einsum(
        "gqkp,ghqk->hp", pair_rep, bias_grads, preferred_element_type=jnp.float32
    )
    modulation_part = jnp.concatenate(
        [
            grad_scale_attn,
            grad_shift_attn,
            grad_gate_attn,
            grad_scale_ff,
            grad_shift_ff,
            grad_gate_ff,
        ],
        axis=1,
    )
    grad_modulation, pair_weight_sum = (
        lax.psum(modulation_part.astype(jnp.bfloat16), "tp").astype(jnp.float32),
        lax.psum(pair_weight_part.astype(jnp.bfloat16), "tp").astype(jnp.float32),
    )
    grad_condition = jnp.dot(grad_modulation, ada_full.T, precision=highest)
    parts = lax.axis_size("dp")
    place = lax.axis_index("dp")
    sizes = [ada_full.shape[1], condition.shape[1], condition.shape[1], onehot.shape[1]]
    chain_rows = jnp.concatenate([grad_modulation, grad_condition, condition, onehot], axis=1)
    packed = jnp.concatenate([chain_rows.reshape(-1), pair_weight_sum.reshape(-1)])
    packed = jnp.pad(packed, (0, -packed.size % 1024)).reshape(-1, 128)
    gathered = lax.all_gather(packed, "dp", axis=0, tiled=True).reshape(parts, -1)
    rows_all = gathered[:, : chain_rows.size].reshape(parts * chains, chain_rows.shape[1])
    pair_all = gathered[:, chain_rows.size : chain_rows.size + pair_weight.size].reshape(
        (parts,) + pair_weight.shape
    )
    cuts = [sum(sizes[:entry]) for entry in range(5)]
    mod_all, grad_cond_all, cond_all, onehot_all = [
        rows_all[:, cuts[entry] : cuts[entry + 1]] for entry in range(4)
    ]

    def own_columns(values, axis):
        width_here = values.shape[axis] // parts
        return lax.dynamic_slice_in_dim(values, place * width_here, width_here, axis)

    grad_ada = jnp.dot(cond_all.T, own_columns(mod_all, 1), precision=highest)
    grad_table = jnp.dot(onehot_all.T, own_columns(grad_cond_all, 1), precision=highest)
    grad_pair_weight = jnp.sum(own_columns(pair_all, 2), axis=0)

    def summed_over_chains(values_list, axes):
        pieces, shapes = ([], [])
        for values, axis in zip(values_list, axes):
            split = (
                values.shape[:axis]
                + (parts, values.shape[axis] // parts)
                + values.shape[axis + 1 :]
            )
            moved = jnp.moveaxis(values.astype(jnp.bfloat16).reshape(split), axis, 0)
            shapes.append(moved.shape[1:])
            pieces.append(moved.reshape(parts, -1, 128))
        joined = jnp.concatenate(pieces, axis=1)
        own = lax.psum_scatter(
            joined.reshape(-1, 128), "dp", scatter_dimension=0, tiled=True
        ).astype(jnp.float32)
        results, start = ([], 0)
        for piece, shape in zip(pieces, shapes):
            results.append(own[start : start + piece.shape[1]].reshape(shape))
            start += piece.shape[1]
        return results

    sum_ff_in, sum_ff_out = summed_over_chains([grad_ff_in, grad_ff_out], [1, 1])
    sum_attn_in, sum_attn_out = summed_over_chains([grad_attn_in, grad_attn_out], [1, 1])
    summed = (
        sum_attn_in,
        sum_attn_out,
        sum_ff_in,
        sum_ff_out,
        grad_ada,
        grad_table,
        grad_pair_weight,
    )
    return (result, grad_inputs, grad_pair) + tuple(summed)


def solution(mesh):
    return jax.shard_map(
        local,
        mesh=mesh,
        in_specs=(
            P("dp", "tp", None),
            P("dp", "tp", None, None),
            P("dp"),
            P("dp"),
            P("dp"),
            P(),
            P(),
            P(),
            P(None, None, "tp"),
            P("tp", None),
            P(None, None, "tp"),
            P("tp", None),
            P("dp", "tp", None),
        ),
        out_specs=(
            P("dp", "tp", None),
            P("dp", "tp", None),
            P("dp", "tp", None, None),
            P(None, "dp", "tp"),
            P("tp", "dp"),
            P(None, "dp", "tp"),
            P("tp", "dp"),
            P(None, "dp"),
            P(None, "dp"),
            P(None, "dp"),
        ),
        check_vma=False,
    )
```

profile of v0, /device:TPU:0, one launch (start us, length us, event | category | flops | bytes accessed | tf_op | source)
XLA Modules:
  0.0 354.6 jit_solution(2040315591612026860)
XLA Ops:
  7.2 11.4 %fusion.11 = bf16[2,12,64,256]{3,1,2,0:T(8,128)(2,1)} fusion(bf16[2,64,256,256]{3,2,1,0:T(8,128)(2,1)} %param.14, bf16[12,256]{1,0:T(8,128)(2,1)} %param.20), kind=kOutput, calls=%fused_computation.33 | convolution fusion | flops 201719808 | bytes 17569792 | tf_op jit(solution)/shard_map/gqkp,hp->ghqk/dot_general | solution.py:76
  21.0 4.2 %all-to-all-start = ((bf16[2,12,64,256]{3,2,0,1:T(8,128)(2,1)}), bf16[2,12,64,256]{3,2,0,1:T(8,128)(2,1)S(1)}, u32[]{:S(2)}, u32[]{:S(2)}) async-start(bf16[2,12,64,256]{3,2,0,1:T(8,128)(2,1)} %copy.89), calls=%async_computation | async-start | bytes 1572864 | tf_op jit(solution)/shard_map/all_to_all | solution.py:79
  29.5 12.4 %all_gather.15 = bf16[2,256,768]{2,1,0:T(8,128)(2,1)S(1)} all-gather(bf16[2,64,768]{2,1,0:T(8,128)(2,1)S(1)} %fusion.41), channel_id=1, replica_groups=mesh['dp'=8,'tp'=4] {'tp'}, dimensions={1}, use_global_device_ids=true | all-gather | bytes 983040 | tf_op jit(solution)/shard_map/all_gather | solution.py:68
  47.0 3.1 copy.92
  56.4 9.2 %all_gather.17 = bf16[2,256,768]{2,1,0:T(8,128)(2,1)} all-gather(bf16[2,64,768]{2,1,0:T(8,128)(2,1)S(1)} %fusion.56), channel_id=1, replica_groups=mesh['dp'=8,'tp'=4] {'tp'}, dimensions={1}, use_global_device_ids=true | all-gather | bytes 983040 | tf_op jit(solution)/shard_map/all_gather | solution.py:119
  65.6 15.1 %reduce-scatter.7.cloned.1.call-done = bf16[2,64,768]{2,1,0:T(8,128)(2,1)} async-done(((bf16[2,256,768]{2,1,0:T(8,128)(2,1)}), bf16[2,64,768]{2,1,0:T(8,128)(2,1)}) %reduce-scatter.7.cloned.1.call-update) | async-done | bytes 196624 | tf_op jit(solution)/shard_map/reduce_scatter | solution.py:98
  84.0 8.0 %all_gather.16 = bf16[2,256,768]{2,1,0:T(8,128)(2,1)S(1)} all-gather(bf16[2,64,768]{2,1,0:T(8,128)(2,1)S(1)} %add_convert_fusion), channel_id=1, replica_groups=mesh['dp'=8,'tp'=4] {'tp'}, dimensions={1}, use_global_device_ids=true | all-gather | bytes 983040 | tf_op jit(solution)/shard_map/all_gather | solution.py:105
  100.2 23.8 %reduce-scatter.11.cloned.1.call-done = bf16[2,64,768]{2,1,0:T(8,128)(2,1)} async-done(((bf16[2,256,768]{2,1,0:T(8,128)(2,1)}), bf16[2,64,768]{2,1,0:T(8,128)(2,1)}) %reduce-scatter.11.cloned.1.call-update) | async-done | bytes 196624 | tf_op jit(solution)/shard_map/reduce_scatter | solution.py:136
  126.9 8.2 %all_gather.18 = bf16[2,256,768]{2,1,0:T(8,128)(2,1)S(1)} all-gather(bf16[2,64,768]{2,1,0:T(8,128)(2,1)S(1)} %multiply_convert_fusion.5), channel_id=1, replica_groups=mesh['dp'=8,'tp'=4] {'tp'}, dimensions={1}, use_global_device_ids=true | all-gather | bytes 983040 | tf_op jit(solution)/shard_map/all_gather | solution.py:144
  142.4 3.3 convolution_convert_fusion.2
  147.1 3.0 fusion.10
  150.2 3.1 reshape.208
  155.3 3.3 reshape.209
  160.1 3.2 bitcast_convert_fusion.1
  165.2 3.0 reshape.218
  172.6 5.5 %reshape.216 = bf16[8,1152,128]{2,1,0:T(8,128)(2,1)} reshape(bf16[8,2,96,768]{3,2,1,0:T(8,128)(2,1)} %bitcast.210) | data formatting | bytes 4718592 | tf_op jit(solution)/shard_map/reshape | solution.py:252
  178.0 3.7 %pad_maximum_fusion = bf16[8,1728,128]{2,1,0:T(8,128)(2,1)} fusion(bf16[8,576,128]{2,1,0:T(8,128)(2,1)S(1)} %copy-done.7, bf16[8,1152,128]{2,1,0:T(8,128)(2,1)} %reshape.216), kind=kLoop, calls=%fused_computation.2 | loop fusion | flops 7077888 | bytes 7077888 | tf_op jit(solution)/shard_map/concatenate | solution.py:253
  183.5 3.5 all-to-all-start.1
  187.2 12.0 %all-to-all-done.1 = bf16[2,3,256,256]{3,0,1,2:T(2,128)(2,1)S(1)} async-done(((bf16[2,3,256,256]{3,0,1,2:T(2,128)(2,1)}), bf16[2,3,256,256]{3,0,1,2:T(2,128)(2,1)S(1)}, u32[]{:S(2)}, u32[]{:S(2)}) %all-to-all-start.1) | async-done | bytes 786464 | tf_op jit(solution)/shard_map/all_to_all | solution.py:195
  199.4 8.3 %fusion.21 = bf16[12,256]{1,0:T(8,128)(2,1)S(1)} fusion(bf16[2,64,256,256]{3,2,1,0:T(8,128)(2,1)} %param.14, bf16[2,12,64,256]{3,2,1,0:T(8,128)(2,1)S(1)} %bitcast.207), kind=kOutput, calls=%fused_computation.48 | convolution fusion | flops 201329664 | bytes 17569792 | tf_op jit(solution)/shard_map/gqkp,ghqk->hp/dot_general | solution.py:199
  207.9 8.6 %convolution_convert_fusion = bf16[2,64,256,256]{3,2,1,0:T(8,128)(2,1)} fusion(bf16[2,12,64,256]{3,2,1,0:T(8,128)(2,1)S(1)} %bitcast.208, bf16[12,256]{1,0:T(8,128)(2,1)S(1)} %copy-done.42), kind=kOutput, calls=%fused_computation | convolution fusion | flops 209715200 | bytes 17569792 | tf_op jit(solution)/shard_map/ghqk,hp->gqkp/dot_general | solution.py:196
  220.0 10.7 %all-reduce.1 = (bf16[3072]{0:T(1024)(128)(2,1)S(1)}, bf16[2,4608]{1,0:T(2,128)(2,1)S(1)}) all-reduce(bf16[3072]{0:T(1024)(128)(2,1)S(1)} %reshape.223, bf16[2,4608]{1,0:T(2,128)(2,1)S(1)} %constant_dynamic-update-slice_fusion), channel_id=1, replica_groups=mesh['dp'=8,'tp'=4] {'tp'}, use_global_device_ids=true, to_apply=%region_24.25 | all-reduce | flops 12288 | bytes 49152 | tf_op jit(solution)/shard_map/psum | solution.py:215
  233.3 32.3 %all_gather.19 = f32[896,128]{1,0:T(8,128)S(1)} all-gather(f32[112,128]{1,0:T(8,128)S(1)} %fusion.73), channel_id=1, replica_groups=mesh['dp'=8,'tp'=4] {'dp'}, dimensions={0}, use_global_device_ids=true | all-gather | bytes 516096 | tf_op jit(solution)/shard_map/all_gather | solution.py:224
  273.6 70.3 %reduce-scatter.17.cloned.1.call-done = bf16[1728,128]{1,0:T(8,128)(2,1)} async-done(((bf16[13824,128]{1,0:T(8,128)(2,1)}), bf16[1728,128]{1,0:T(8,128)(2,1)}) %reduce-scatter.17.cloned.1.call-update) | async-done | bytes 442384 | tf_op jit(solution)/shard_map/reduce_scatter | solution.py:254
  (237 shorter events, 70.4 us)
Async XLA Ops:
  7.2 85.8 %copy-start = (bf16[2,768,768]{2,1,0:T(8,128)(2,1)S(1)}, bf16[2,768,768]{2,1,0:T(8,128)(2,1)}, u32[]{:S(2)}) copy-start(bf16[2,768,768]{2,1,0:T(8,128)(2,1)} %param.23) | copy-start | bytes 7077892
  21.0 24.4 %all-to-all-start = ((bf16[2,12,64,256]{3,2,0,1:T(8,128)(2,1)}), bf16[2,12,64,256]{3,2,0,1:T(8,128)(2,1)S(1)}, u32[]{:S(2)}, u32[]{:S(2)}) async-start(bf16[2,12,64,256]{3,2,0,1:T(8,128)(2,1)} %copy.89), calls=%async_computation | async-start | bytes 1572864 | tf_op jit(solution)/shard_map/all_to_all | solution.py:79
  25.2 55.5 %reduce-scatter.7.cloned.1.call-start = ((), (), s32[]{:S(2)}) async-start(), calls=%async_computation.8 | async-start | bytes 983040 | tf_op jit(solution)/shard_map/reduce_scatter | solution.py:98
  25.6 16.3 %copy-start.46 = (f32[2,64]{1,0:T(2,128)}, f32[2,64]{1,0:T(2,128)S(1)}, u32[]{:S(2)}) copy-start(f32[2,64]{1,0:T(2,128)S(1)} %add_rsqrt_fusion.1) | copy-start | bytes 1540
  25.9 16.0 %copy-start.58 = (s32[2]{0:T(128)S(1)}, s32[2]{0:T(128)}, u32[]{:S(2)}) copy-start(s32[2]{0:T(128)} %param.17) | copy-start | bytes 28
  25.9 16.7 %copy-start.23 = (bf16[4,768,192]{1,2,0:T(8,128)(2,1)S(1)}, bf16[4,768,192]{1,2,0:T(8,128)(2,1)}, u32[]{:S(2)}) copy-start(bf16[4,768,192]{1,2,0:T(8,128)(2,1)} %param.21) | copy-start | bytes 3538948
  29.3 12.6 %copy-start.34 = (f32[2,768]{1,0:T(2,128)}, f32[2,768]{1,0:T(2,128)S(1)}, u32[]{:S(2)}) copy-start(f32[2,768]{1,0:T(2,128)S(1)} %get-tuple-element.76) | copy-start | bytes 18436
  55.0 10.6 %copy-start.14 = (bf16[2,256,192]{1,2,0:T(8,128)(2,1)}, bf16[2,256,192]{1,2,0:T(8,128)(2,1)S(1)}, u32[]{:S(2)}) copy-start(bf16[2,256,192]{1,2,0:T(8,128)(2,1)S(1)} %fusion.62) | copy-start | bytes 589828
  56.3 26.7 %copy-start.45 = (f32[2,768]{1,0:T(2,128)S(1)}, f32[2,768]{1,0:T(2,128)}, u32[]{:S(2)}) copy-start(f32[2,768]{1,0:T(2,128)} %get-tuple-element.73) | copy-start | bytes 18436
  56.3 67.7 %reduce-scatter.11.cloned.1.call-start = ((), (), s32[]{:S(2)}) async-start(), calls=%async_computation.10 | async-start | bytes 983040 | tf_op jit(solution)/shard_map/reduce_scatter | solution.py:136
  81.8 43.4 %copy-start.38 = (f32[2,64]{1,0:T(2,128)}, f32[2,64]{1,0:T(2,128)S(1)}, u32[]{:S(2)}) copy-start(f32[2,64]{1,0:T(2,128)S(1)} %broadcast_multiply_fusion.4) | copy-start | bytes 1540
  82.9 42.3 %copy-start.40 = (f32[2,64]{1,0:T(2,128)}, f32[2,64]{1,0:T(2,128)S(1)}, u32[]{:S(2)}) copy-start(f32[2,64]{1,0:T(2,128)S(1)} %add_rsqrt_fusion) | copy-start | bytes 1540
  97.8 26.3 %copy-start.5 = (bf16[2,64,768]{2,1,0:T(8,128)(2,1)S(1)}, bf16[2,64,768]{2,1,0:T(8,128)(2,1)}, u32[]{:S(2)}) copy-start(bf16[2,64,768]{2,1,0:T(8,128)(2,1)} %reduce-scatter.7.cloned.1.call-done) | copy-start | bytes 589828
  100.1 35.0 %copy-start.22 = (f32[2,3,64,256]{3,2,1,0:T(8,128)S(1)}, f32[2,3,64,256]{3,2,1,0:T(8,128)}, u32[]{:S(2)}) copy-start(f32[2,3,64,256]{3,2,1,0:T(8,128)} %copy-done.21) | copy-start | bytes 1179652
  100.1 116.3 %reduce-scatter.13.cloned.1.call-start = ((), (), s32[]{:S(2)}) async-start(), calls=%async_computation.11 | async-start | bytes 983040 | tf_op jit(solution)/shard_map/reduce_scatter | solution.py:187
  142.3 75.2 %reduce-scatter.9.cloned.1.call-start = ((), (), s32[]{:S(2)}) async-start(), calls=%async_computation.9 | async-start | bytes 983040 | tf_op jit(solution)/shard_map/reduce_scatter | solution.py:111
  145.7 124.6 %reduce-scatter.15.cloned.1.call-start = ((), (), s32[]{:S(2)}) async-start(), calls=%async_computation.12 | async-start | bytes 1658880 | tf_op jit(solution)/shard_map/reduce_scatter | solution.py:254
  159.8 184.0 %reduce-scatter.17.cloned.1.call-start = ((), (), s32[]{:S(2)}) async-start(), calls=%async_computation.13 | async-start | bytes 3981312 | tf_op jit(solution)/shard_map/reduce_scatter | solution.py:254
  183.5 15.7 %all-to-all-start.1 = ((bf16[2,3,256,256]{3,0,1,2:T(2,128)(2,1)}), bf16[2,3,256,256]{3,0,1,2:T(2,128)(2,1)S(1)}, u32[]{:S(2)}, u32[]{:S(2)}) async-start(bf16[2,3,256,256]{3,0,1,2:T(2,128)(2,1)} %copy.98), calls=%async_computation.5 | async-start | bytes 1572864 | tf_op jit(solution)/shard_map/all_to_all | solution.py:195
  207.8 9.7 %copy-start.9 = (bf16[2,64,768]{2,1,0:T(8,128)(2,1)S(1)}, bf16[2,64,768]{2,1,0:T(8,128)(2,1)}, u32[]{:S(2)}) copy-start(bf16[2,64,768]{2,1,0:T(8,128)(2,1)} %param.25) | copy-start | bytes 589828
  207.8 9.7 %copy-start.35 = (f32[2,768]{1,0:T(2,128)S(1)}, f32[2,768]{1,0:T(2,128)}, u32[]{:S(2)}) copy-start(f32[2,768]{1,0:T(2,128)} %copy-done.34) | copy-start | bytes 18436
  207.8 9.7 %copy-start.37 = (f32[2,768]{1,0:T(2,128)S(1)}, f32[2,768]{1,0:T(2,128)}, u32[]{:S(2)}) copy-start(f32[2,768]{1,0:T(2,128)} %get-tuple-element.72) | copy-start | bytes 18436
  207.8 9.7 %copy-start.39 = (f32[2,64]{1,0:T(2,128)S(1)}, f32[2,64]{1,0:T(2,128)}, u32[]{:S(2)}) copy-start(f32[2,64]{1,0:T(2,128)} %copy-done.38) | copy-start | bytes 1540
  219.9 13.2 %copy-start.53 = (f32[2,256]{1,0:T(2,128)S(1)}, f32[2,256]{1,0:T(2,128)}, u32[]{:S(2)}) copy-start(f32[2,256]{1,0:T(2,128)} %copy-done.52) | copy-start | bytes 6148
  (48 other events, 180.4 us)
Sparse Core Ops, SparseCore 0:
  56.4 24.2 reduce-scatter.6
  100.2 23.7 reduce-scatter.10
  142.4 23.7 reduce-scatter.12
  168.6 23.7 reduce-scatter.8
  195.8 65.7 reduce-scatter.14
  265.1 78.7 reduce-scatter.16
where the time goes:
time: 356 us; the launch traced here: 355 us
  waiting for transfers between devices  121 us (34%)
  blocking collectives  80.8 us (23%)
  matrix products  65.1 us (18%)
  local copies, waits for them, and re-layouts  44.4 us (12%)
  other arithmetic  19.8 us (6%)
  between operations  15 us (4%)
  starting transfers between devices  8.16 us (2%)
    reduce_scatter x2, waiting for transfers between devices, summed_over_chains(): lax.psum_scatter(joined.reshape(-1, 128), 'dp', scatter_dimension=0, tile...  70.3 us
    all_gather x1, blocking collectives, local(): lax.all_gather(packed, 'dp', axis=0, tiled=True).reshape(parts, -1)  32.3 us
    reduce_scatter x1, waiting for transfers between devices, local(): lax.psum_scatter(ff_row_terms.astype(jnp.bfloat16), 'tp', scatter_dimensi...  23.8 us
    reduce_scatter x1, waiting for transfers between devices, local(): lax.psum_scatter(attn_terms.astype(jnp.bfloat16), 'tp', scatter_dimension...  15.1 us
    all_gather x1, blocking collectives, local(): gathered_attn = lax.all_gather(rows_attn, 'tp', axis=1, tiled=True)  12.4 us
    reshape x4, local copies, waits for them, and re-layouts, summed_over_chains(): pieces.append(moved.reshape(parts, -1, 128))  12.3 us
    all_to_all x1, waiting for transfers between devices, local(): lax.all_to_all(grad_scores, 'tp', split_axis=2, concat_axis=1, tiled=True)  12 us
    dot_general x1, matrix products, local(): jnp.einsum('gqkp,hp->ghqk', pair_rep, pair_weight, preferred_element_type...  11.4 us
  transfers between devices with their start and end apart: 8, of which 4 were waited for; matrix products, arithmetic and copies ran while one was open for 22% of the time, Pallas kernels for 0%

commit v1 on v0

--- a/solution.py
+++ b/solution.py
@@ -5,6 +5,23 @@
 from jax.sharding import PartitionSpec as P
 
 highest = lax.Precision.HIGHEST
+
+
+def in_order(parts, dim):
+    parts = jnp.moveaxis(parts, 0, dim)
+    lengths = parts.shape
+    return parts.reshape(*lengths[:dim], lengths[dim] * lengths[dim + 1], *lengths[dim + 2 :])
+
+
+def grow_blocks(array, axis):
+    peers, index = (lax.axis_size(axis), lax.axis_index(axis))
+    pieces, apart = (array[None], 1)
+    while apart < peers:
+        theirs = lax.ppermute(pieces, axis, [(i, i ^ apart) for i in range(peers)])
+        low = index & apart == 0
+        pieces = jnp.concatenate([jnp.where(low, pieces, theirs), jnp.where(low, theirs, pieces)])
+        apart *= 2
+    return pieces
 
 
 def time_features(noise_times, cond_width):
@@ -102,7 +119,7 @@
     middle = inputs_full + sig_attn * attended
     normed_ff, inverse_ff = normalize(middle)
     rows_ff = (normed_ff * (1.0 + scale_ff) + shift_ff).astype(jnp.bfloat16)
-    gathered_ff = lax.all_gather(rows_ff, "tp", axis=1, tiled=True)
+    gathered_ff = in_order(grow_blocks(rows_ff, "tp"), 1)
     gate_up = jnp.einsum("gld,kdf->kglf", gathered_ff, ff_in, preferred_element_type=jnp.float32)
     sig_hidden = jax.nn.sigmoid(gate_up[0])
     silu_hidden = gate_up[0] * sig_hidden

time: 356 us -> 368 us (1.034)
  waiting for transfers between devices: 121 us -> 131 us
    reduce_scatter x1, waiting for transfers between devices: 15.1 us -> 24.3 us  [local(): lax.psum_scatter(attn_terms.astype(jnp.bfloat16), 'tp', scatter_dimension...]
    all_gather x1 -> x0, blocking collectives: 8.02 us -> none  [local(): gathered_ff = lax.all_gather(rows_ff, 'tp', axis=1, tiled=True)]
    all_gather x1, blocking collectives: 9.17 us -> 15.4 us  [local(): gathered_grad_ff = lax.all_gather(grad_trans, 'tp', axis=1, tiled=True)]
    unnamed x133 -> x135, local copies, waits for them, and re-layouts: 6.75 us -> 7.95 us
  transfers between devices with their start and end apart: 8 -> 10, of which waited for: 4 -> 5; matrix products, arithmetic and copies ran while one was open for 22% -> 22% of each run, Pallas kernels for 0% -> 0%
where the time goes in v1:
time: 368 us; the launch traced here: 367 us
  waiting for transfers between devices  131 us (36%)
  blocking collectives  78.6 us (21%)
  matrix products  65.1 us (18%)
  local copies, waits for them, and re-layouts  45.6 us (12%)
  other arithmetic  22.7 us (6%)
  between operations  15 us (4%)
  starting transfers between devices  8.56 us (2%)
    reduce_scatter x2, waiting for transfers between devices, summed_over_chains(): lax.psum_scatter(joined.reshape(-1, 128), 'dp', scatter_dimension=0, tile...  69.9 us
    all_gather x1, blocking collectives, local(): lax.all_gather(packed, 'dp', axis=0, tiled=True).reshape(parts, -1)  32.5 us
    reduce_scatter x1, waiting for transfers between devices, local(): lax.psum_scatter(attn_terms.astype(jnp.bfloat16), 'tp', scatter_dimension...  24.3 us
    reduce_scatter x1, waiting for transfers between devices, local(): lax.psum_scatter(ff_row_terms.astype(jnp.bfloat16), 'tp', scatter_dimensi...  23.3 us
    all_gather x1, blocking collectives, local(): gathered_grad_ff = lax.all_gather(grad_trans, 'tp', axis=1, tiled=True)  15.4 us
    reshape x4, local copies, waits for them, and re-layouts, summed_over_chains(): pieces.append(moved.reshape(parts, -1, 128))  12.2 us
    all_to_all x1, waiting for transfers between devices, local(): lax.all_to_all(grad_scores, 'tp', split_axis=2, concat_axis=1, tiled=True)  12 us
    all_gather x1, blocking collectives, local(): gathered_attn = lax.all_gather(rows_attn, 'tp', axis=1, tiled=True)  11.8 us
  transfers between devices with their start and end apart: 10, of which 5 were waited for; matrix products, arithmetic and copies ran while one was open for 22% of the time, Pallas kernels for 0%

profile of v1, /device:TPU:0, one launch (start us, length us, event | category | flops | bytes accessed | tf_op | source)
XLA Modules:
  0.0 366.7 jit_solution(7462585703910938950)
XLA Ops:
  7.2 11.4 %fusion.11 = bf16[2,12,64,256]{3,1,2,0:T(8,128)(2,1)} fusion(bf16[2,64,256,256]{3,2,1,0:T(8,128)(2,1)} %param.14, bf16[12,256]{1,0:T(8,128)(2,1)} %param.20), kind=kOutput, calls=%fused_computation.33 | convolution fusion | flops 201719808 | bytes 17569792 | tf_op jit(solution)/shard_map/gqkp,hp->ghqk/dot_general | solution.py:93
  21.0 4.2 %all-to-all-start = ((bf16[2,12,64,256]{3,2,0,1:T(8,128)(2,1)}), bf16[2,12,64,256]{3,2,0,1:T(8,128)(2,1)S(1)}, u32[]{:S(2)}, u32[]{:S(2)}) async-start(bf16[2,12,64,256]{3,2,0,1:T(8,128)(2,1)} %copy.96), calls=%async_computation | async-start | bytes 1572864 | tf_op jit(solution)/shard_map/all_to_all | solution.py:96
  30.1 11.8 %all_gather.12 = bf16[2,256,768]{2,1,0:T(8,128)(2,1)S(1)} all-gather(bf16[2,64,768]{2,1,0:T(8,128)(2,1)S(1)} %fusion.39), channel_id=1, replica_groups=mesh['dp'=8,'tp'=4] {'tp'}, dimensions={1}, use_global_device_ids=true | all-gather | bytes 983040 | tf_op jit(solution)/shard_map/all_gather | solution.py:85
  47.0 3.1 copy.99
  57.1 24.3 %reduce-scatter.7.cloned.1.call-done = bf16[2,64,768]{2,1,0:T(8,128)(2,1)} async-done(((bf16[2,256,768]{2,1,0:T(8,128)(2,1)}), bf16[2,64,768]{2,1,0:T(8,128)(2,1)}) %reduce-scatter.7.cloned.1.call-update) | async-done | bytes 196624 | tf_op jit(solution)/shard_map/reduce_scatter | solution.py:115
  88.1 15.4 %all_gather.13 = bf16[2,256,768]{2,1,0:T(8,128)(2,1)S(1)} all-gather(bf16[2,64,768]{2,1,0:T(8,128)(2,1)S(1)} %fusion.54), channel_id=1, replica_groups=mesh['dp'=8,'tp'=4] {'tp'}, dimensions={1}, use_global_device_ids=true | all-gather | bytes 983040 | tf_op jit(solution)/shard_map/all_gather | solution.py:136
  113.0 23.3 %reduce-scatter.11.cloned.1.call-done = bf16[2,64,768]{2,1,0:T(8,128)(2,1)} async-done(((bf16[2,256,768]{2,1,0:T(8,128)(2,1)}), bf16[2,64,768]{2,1,0:T(8,128)(2,1)}) %reduce-scatter.11.cloned.1.call-update) | async-done | bytes 196624 | tf_op jit(solution)/shard_map/reduce_scatter | solution.py:153
  139.2 8.2 %all_gather.14 = bf16[2,256,768]{2,1,0:T(8,128)(2,1)S(1)} all-gather(bf16[2,64,768]{2,1,0:T(8,128)(2,1)S(1)} %multiply_convert_fusion.5), channel_id=1, replica_groups=mesh['dp'=8,'tp'=4] {'tp'}, dimensions={1}, use_global_device_ids=true | all-gather | bytes 983040 | tf_op jit(solution)/shard_map/all_gather | solution.py:161
  154.7 3.3 convolution_convert_fusion.2
  159.5 3.1 fusion.10
  162.5 3.1 reshape.212
  167.7 3.3 reshape.213
  172.5 3.2 bitcast_convert_fusion.1
  177.5 3.0 reshape.222
  180.5 2.8 bitcast_convert_fusion
  184.9 5.4 %reshape.220 = bf16[8,1152,128]{2,1,0:T(8,128)(2,1)} reshape(bf16[8,2,96,768]{3,2,1,0:T(8,128)(2,1)} %bitcast.215) | data formatting | bytes 4718592 | tf_op jit(solution)/shard_map/reshape | solution.py:269
  190.4 3.7 pad_maximum_fusion
  195.9 3.5 all-to-all-start.1
  199.5 12.0 %all-to-all-done.1 = bf16[2,3,256,256]{3,0,1,2:T(2,128)(2,1)S(1)} async-done(((bf16[2,3,256,256]{3,0,1,2:T(2,128)(2,1)}), bf16[2,3,256,256]{3,0,1,2:T(2,128)(2,1)S(1)}, u32[]{:S(2)}, u32[]{:S(2)}) %all-to-all-start.1) | async-done | bytes 786464 | tf_op jit(solution)/shard_map/all_to_all | solution.py:212
  211.7 8.3 %fusion.21 = bf16[12,256]{1,0:T(8,128)(2,1)S(1)} fusion(bf16[2,64,256,256]{3,2,1,0:T(8,128)(2,1)} %param.14, bf16[2,12,64,256]{3,2,1,0:T(8,128)(2,1)S(1)} %bitcast.212), kind=kOutput, calls=%fused_computation.48 | convolution fusion | flops 201329664 | bytes 17569792 | tf_op jit(solution)/shard_map/gqkp,ghqk->hp/dot_general | solution.py:216
  220.2 8.6 %convolution_convert_fusion = bf16[2,64,256,256]{3,2,1,0:T(8,128)(2,1)} fusion(bf16[2,12,64,256]{3,2,1,0:T(8,128)(2,1)S(1)} %bitcast.213, bf16[12,256]{1,0:T(8,128)(2,1)S(1)} %copy-done.43), kind=kOutput, calls=%fused_computation | convolution fusion | flops 209715200 | bytes 17569792 | tf_op jit(solution)/shard_map/ghqk,hp->gqkp/dot_general | solution.py:213
  232.3 10.7 %all-reduce.1 = (bf16[3072]{0:T(1024)(128)(2,1)S(1)}, bf16[2,4608]{1,0:T(2,128)(2,1)S(1)}) all-reduce(bf16[3072]{0:T(1024)(128)(2,1)S(1)} %reshape.227, bf16[2,4608]{1,0:T(2,128)(2,1)S(1)} %constant_dynamic-update-slice_fusion), channel_id=1, replica_groups=mesh['dp'=8,'tp'=4] {'tp'}, use_global_device_ids=true, to_apply=%region_24.25 | all-reduce | flops 12288 | bytes 49152 | tf_op jit(solution)/shard_map/psum | solution.py:232
  245.6 32.5 %all_gather.15 = f32[896,128]{1,0:T(8,128)S(1)} all-gather(f32[112,128]{1,0:T(8,128)S(1)} %fusion.72), channel_id=1, replica_groups=mesh['dp'=8,'tp'=4] {'dp'}, dimensions={0}, use_global_device_ids=true | all-gather | bytes 516096 | tf_op jit(solution)/shard_map/all_gather | solution.py:241
  286.1 69.9 %reduce-scatter.17.cloned.1.call-done = bf16[1728,128]{1,0:T(8,128)(2,1)} async-done(((bf16[13824,128]{1,0:T(8,128)(2,1)}), bf16[1728,128]{1,0:T(8,128)(2,1)}) %reduce-scatter.17.cloned.1.call-update) | async-done | bytes 442384 | tf_op jit(solution)/shard_map/reduce_scatter | solution.py:271
  (247 shorter events, 73.6 us)
Async XLA Ops:
  7.2 98.7 %copy-start = (bf16[2,768,768]{2,1,0:T(8,128)(2,1)S(1)}, bf16[2,768,768]{2,1,0:T(8,128)(2,1)}, u32[]{:S(2)}) copy-start(bf16[2,768,768]{2,1,0:T(8,128)(2,1)} %param.23) | copy-start | bytes 7077892
  21.0 24.4 %all-to-all-start = ((bf16[2,12,64,256]{3,2,0,1:T(8,128)(2,1)}), bf16[2,12,64,256]{3,2,0,1:T(8,128)(2,1)S(1)}, u32[]{:S(2)}, u32[]{:S(2)}) async-start(bf16[2,12,64,256]{3,2,0,1:T(8,128)(2,1)} %copy.96), calls=%async_computation | async-start | bytes 1572864 | tf_op jit(solution)/shard_map/all_to_all | solution.py:96
  25.2 56.2 %reduce-scatter.7.cloned.1.call-start = ((), (), s32[]{:S(2)}) async-start(), calls=%async_computation.8 | async-start | bytes 983040 | tf_op jit(solution)/shard_map/reduce_scatter | solution.py:115
  25.6 16.3 %copy-start.47 = (f32[2,64]{1,0:T(2,128)}, f32[2,64]{1,0:T(2,128)S(1)}, u32[]{:S(2)}) copy-start(f32[2,64]{1,0:T(2,128)S(1)} %add_rsqrt_fusion.1) | copy-start | bytes 1540
  26.5 15.4 %copy-start.59 = (s32[2]{0:T(128)S(1)}, s32[2]{0:T(128)}, u32[]{:S(2)}) copy-start(s32[2]{0:T(128)} %param.17) | copy-start | bytes 28
  26.5 16.2 %copy-start.23 = (bf16[4,768,192]{1,2,0:T(8,128)(2,1)S(1)}, bf16[4,768,192]{1,2,0:T(8,128)(2,1)}, u32[]{:S(2)}) copy-start(bf16[4,768,192]{1,2,0:T(8,128)(2,1)} %param.21) | copy-start | bytes 3538948
  29.9 14.7 %copy-start.34 = (f32[2,768]{1,0:T(2,128)}, f32[2,768]{1,0:T(2,128)S(1)}, u32[]{:S(2)}) copy-start(f32[2,768]{1,0:T(2,128)S(1)} %get-tuple-element.80) | copy-start | bytes 18436
  55.7 28.0 %copy-start.46 = (f32[2,768]{1,0:T(2,128)S(1)}, f32[2,768]{1,0:T(2,128)}, u32[]{:S(2)}) copy-start(f32[2,768]{1,0:T(2,128)} %get-tuple-element.77) | copy-start | bytes 18436
  57.0 30.4 %copy-start.8 = (bf16[2,64,768]{2,1,0:T(8,128)(2,1)S(1)}, bf16[2,64,768]{2,1,0:T(8,128)(2,1)}, u32[]{:S(2)}) copy-start(bf16[2,64,768]{2,1,0:T(8,128)(2,1)} %param.25) | copy-start | bytes 589828
  57.0 79.3 %reduce-scatter.11.cloned.1.call-start = ((), (), s32[]{:S(2)}) async-start(), calls=%async_computation.10 | async-start | bytes 983040 | tf_op jit(solution)/shard_map/reduce_scatter | solution.py:153
  84.7 1.5 collective-permute-start
  87.1 16.5 %collective-permute-start.1 = (bf16[2,2,64,768]{3,2,1,0:T(8,128)(2,1)}, bf16[2,2,64,768]{3,2,1,0:T(8,128)(2,1)}, u32[]{:S(2)}, u32[]{:S(2)}) collective-permute-start(bf16[2,2,64,768]{3,2,1,0:T(8,128)(2,1)} %pad_maximum_fusion.6), channel_id=1, source_target_pairs={{0,2},{1,3},{2,0},{3,1},{4,6},{5,7},{6,4},{7,5},{8,10},{9,11},{10,... | collective-permute-start | bytes 1179656 | tf_op jit(solution)/shard_map/ppermute | solution.py:20
  110.6 25.7 %copy-start.5 = (bf16[2,64,768]{2,1,0:T(8,128)(2,1)S(1)}, bf16[2,64,768]{2,1,0:T(8,128)(2,1)}, u32[]{:S(2)}) copy-start(bf16[2,64,768]{2,1,0:T(8,128)(2,1)} %reduce-scatter.7.cloned.1.call-done) | copy-start | bytes 589828
  110.6 25.7 %copy-start.38 = (f32[2,64]{1,0:T(2,128)S(1)}, f32[2,64]{1,0:T(2,128)}, u32[]{:S(2)}) copy-start(f32[2,64]{1,0:T(2,128)} %copy-done.37) | copy-start | bytes 1540
  110.6 25.7 %copy-start.41 = (f32[2,64]{1,0:T(2,128)S(1)}, f32[2,64]{1,0:T(2,128)}, u32[]{:S(2)}) copy-start(f32[2,64]{1,0:T(2,128)} %copy-done.40) | copy-start | bytes 1540
  112.9 34.5 %copy-start.22 = (f32[2,3,64,256]{3,2,1,0:T(8,128)S(1)}, f32[2,3,64,256]{3,2,1,0:T(8,128)}, u32[]{:S(2)}) copy-start(f32[2,3,64,256]{3,2,1,0:T(8,128)} %copy-done.21) | copy-start | bytes 1179652
  113.0 115.8 %reduce-scatter.13.cloned.1.call-start = ((), (), s32[]{:S(2)}) async-start(), calls=%async_computation.11 | async-start | bytes 983040 | tf_op jit(solution)/shard_map/reduce_scatter | solution.py:204
  154.6 75.1 %reduce-scatter.9.cloned.1.call-start = ((), (), s32[]{:S(2)}) async-start(), calls=%async_computation.9 | async-start | bytes 983040 | tf_op jit(solution)/shard_map/reduce_scatter | solution.py:128
  158.0 124.7 %reduce-scatter.15.cloned.1.call-start = ((), (), s32[]{:S(2)}) async-start(), calls=%async_computation.12 | async-start | bytes 1658880 | tf_op jit(solution)/shard_map/reduce_scatter | solution.py:271
  172.2 183.8 %reduce-scatter.17.cloned.1.call-start = ((), (), s32[]{:S(2)}) async-start(), calls=%async_computation.13 | async-start | bytes 3981312 | tf_op jit(solution)/shard_map/reduce_scatter | solution.py:271
  195.9 15.7 %all-to-all-start.1 = ((bf16[2,3,256,256]{3,0,1,2:T(2,128)(2,1)}), bf16[2,3,256,256]{3,0,1,2:T(2,128)(2,1)S(1)}, u32[]{:S(2)}, u32[]{:S(2)}) async-start(bf16[2,3,256,256]{3,0,1,2:T(2,128)(2,1)} %copy.106), calls=%async_computation.5 | async-start | bytes 1572864 | tf_op jit(solution)/shard_map/all_to_all | solution.py:212
  220.1 9.7 %copy-start.9 = (bf16[2,64,768]{2,1,0:T(8,128)(2,1)S(1)}, bf16[2,64,768]{2,1,0:T(8,128)(2,1)}, u32[]{:S(2)}) copy-start(bf16[2,64,768]{2,1,0:T(8,128)(2,1)} %param.25) | copy-start | bytes 589828
  220.1 9.7 %copy-start.35 = (f32[2,768]{1,0:T(2,128)S(1)}, f32[2,768]{1,0:T(2,128)}, u32[]{:S(2)}) copy-start(f32[2,768]{1,0:T(2,128)} %copy-done.34) | copy-start | bytes 18436
  232.2 13.2 %copy-start.54 = (f32[2,256]{1,0:T(2,128)S(1)}, f32[2,256]{1,0:T(2,128)}, u32[]{:S(2)}) copy-start(f32[2,256]{1,0:T(2,128)} %copy-done.53) | copy-start | bytes 6148
  (51 other events, 198.2 us)
Sparse Core Ops, SparseCore 0:
  57.2 24.2 reduce-scatter.6
  113.1 23.1 reduce-scatter.10
  154.7 23.7 reduce-scatter.12
  180.9 23.7 reduce-scatter.8
  208.1 65.7 reduce-scatter.14
  277.4 78.5 reduce-scatter.16
